TPU v7x, 32 devices: a whole 2x2x4 slice. The times are simulated.
32 devices in a mesh: dp: 8 (over z, x), mp: 4 (over y, core).
Axes of the slice: x: 2, y: 2, z: 4, core: 2. Of those that a mesh axis runs over, the one named last changes fastest.
Arguments:
- hidden_in: bfloat16 [2, 1024, 3584], P(None, 'dp', 'mp'), may hold values from -6 to 6
- out_grad: bfloat16 [2, 1024, 3584], P(None, 'dp', 'mp'), may hold values from -1536 to 1536
- pack_fill: int32 [2, 8], P(None, 'dp'), may hold values from 1 to 128, as said below
- norm_gain: float32 [3584], P('mp'), may hold values from 0.5 to 1.5
- up_weight: bfloat16 [3584, 7168], P(None, 'mp'), may hold values from -0.09375 to 0.09375
- down_weight: bfloat16 [7168, 3584], P('mp'), may hold values from -0.0625 to 0.0625
Outputs:
- in_grad: bfloat16 [2, 1024, 3584], P(None, 'dp', 'mp')
- up_grad: float32 [3584, 7168], P('dp', 'mp')
- down_grad: float32 [7168, 3584], P('mp', 'dp')
- gain_grad: float32 [3584], P('mp')
Inputs may be any that keep to these rules, and one draw needn't show every extreme that they name: pack_fill[m, p] real tokens stand at the start of pack p of microbatch m (positions p * 128 onward); the other positions of the pack are padding and carry no loss. In every draw the last pack of the first microbatch is full.
All inputs are finite; a program needn't handle non-finite values.
Results may differ from a plain program's by a relative error of at most 0.014.
Values may be sent and summed in bfloat16 or wider, within the bound.
A program may use at most 128 MiB of HBM per device.

v0:
```python
import functools

import jax
import jax.numpy as jnp
from jax import lax
from jax.experimental import pallas as pl
from jax.experimental.pallas import tpu as pltpu
from jax.sharding import PartitionSpec as P


epsilon = 1e-06


def gelu_tanh(value):
    return jax.nn.gelu(value, approximate=True)


def contract_rows(left, right):
    return lax.dot_general(
        left, right, (((0,), (0,)), ((), ())), preferred_element_type=jnp.float32
    )


def contract_cols(left, right):
    return lax.dot_general(
        left, right, (((1,), (1,)), ((), ())), preferred_element_type=jnp.float32
    )


def stripe(rows, n_dp):
    micro, tok, width = rows.shape
    parts = []
    for m in range(micro):
        part = rows[m].reshape(tok // n_dp, n_dp, width).transpose(1, 0, 2)
        parts.append(part[::-1] if m % 2 else part)
    return jnp.concatenate(parts, axis=1)


def unstripe(slots, micro):
    n_dp, per, width = slots.shape
    share = per // micro
    outs = []
    for m in range(micro):
        part = slots[:, m * share : (m + 1) * share]
        part = part[::-1] if m % 2 else part
        outs.append(part.transpose(1, 0, 2).reshape(share * n_dp, width))
    return jnp.stack(outs)


def flipped(index, bit):
    return index + bit - 2 * bit * lax.rem(lax.div(index, bit), 2)


def flipped_by(index, mask):
    bit = 1
    while bit <= mask:
        if mask & bit:
            index = flipped(index, bit)
        bit *= 2
    return index


def exchange_kernel(axes, *refs):
    count = len(axes)
    ins, outs = refs[:count], refs[count : 2 * count]
    sems = refs[2 * count :]
    barrier = pltpu.get_barrier_semaphore()
    greeted = 0
    for axis in sorted({axis for axis, _ in axes}):
        n, me = lax.axis_size(axis), lax.axis_index(axis)
        for d in range(1, n):
            pl.semaphore_signal(
                barrier,
                inc=1,
                device_id={axis: lax.rem(me + d, n)},
                device_id_type=pl.DeviceIdType.MESH,
            )
        greeted += n - 1
    pl.semaphore_wait(barrier, greeted)

    def send(k, axis, source, target, peer, slot):
        copy = pltpu.make_async_remote_copy(
            src_ref=source,
            dst_ref=outs[k].at[target],
            send_sem=sems[2 * k].at[slot],
            recv_sem=sems[2 * k + 1].at[slot],
            device_id={axis: peer},
            device_id_type=pl.DeviceIdType.MESH,
        )
        copy.start()
        return copy

    trees = [k for k, (_, kind) in enumerate(axes) if kind == "tree"]
    copies = {}

    def forward(k, mask, below):
        axis = axes[k][0]
        me = lax.axis_index(axis)
        owner = flipped_by(me, mask)
        bit = below
        while bit >= 1:
            copies[k, mask ^ bit] = send(
                k,
                axis,
                outs[k].at[owner] if mask else ins[k],
                owner,
                flipped(me, bit),
                mask ^ bit,
            )
            bit //= 2

    for k in trees:
        forward(k, 0, lax.axis_size(axes[k][0]) // 2)
    locals_ = []
    for k, (axis, kind) in enumerate(axes):
        n, me = lax.axis_size(axis), lax.axis_index(axis)
        for d in [n // 2] + [d for d in range(1, n) if d != n // 2]:
            if kind == "tree":
                break
            peer = lax.rem(me + d, n)
            source = ins[k].at[peer] if kind == "split" else ins[k]
            copies[k, d] = send(k, axis, source, me, peer, d)
        own = pltpu.make_async_copy(
            ins[k].at[me] if kind == "split" else ins[k],
            outs[k].at[me],
            sems[2 * k].at[0],
        )
        own.start()
        locals_.append(own)
    relayed = set()
    if trees:
        n = lax.axis_size(axes[trees[0]][0])
        for mask in sorted(range(2, n, 2), key=lambda m: (bin(m).count("1"), -m)):
            for k in trees:
                copies[k, mask].wait_recv()
                relayed.add((k, mask))
                forward(k, mask, (mask & -mask) // 2)
    for key, copy in copies.items():
        copy.wait_send()
        if key not in relayed:
            copy.wait_recv()
    for own in locals_:
        own.wait()


def exchange(arrays, axes, collective_id):
    shapes, sems = [], []
    for array, (axis, kind) in zip(arrays, axes):
        n = lax.axis_size(axis)
        block = array.shape[1:] if kind == "split" else array.shape
        shapes.append(jax.ShapeDtypeStruct((n,) + block, array.dtype))
        sems += [pltpu.SemaphoreType.DMA((n,)), pltpu.SemaphoreType.DMA((n,))]
    vmem = pl.BlockSpec(memory_space=pltpu.VMEM)
    return pl.pallas_call(
        functools.partial(exchange_kernel, axes),
        out_shape=shapes,
        in_specs=[vmem] * len(arrays),
        out_specs=[vmem] * len(arrays),
        scratch_shapes=sems,
        compiler_params=pltpu.CompilerParams(
            collective_id=collective_id, has_side_effects=True
        ),
    )(*arrays)


def on_device(hidden_in, out_grad, pack_fill, norm_gain, up_weight, down_weight):
    micro, tok, width = hidden_in.shape
    model_width, ff_shard = up_weight.shape
    n_dp, n_mp = lax.axis_size("dp"), lax.axis_size("mp")
    me = lax.axis_index("dp")
    share = tok // n_dp
    slot_count = n_dp * micro * share
    chunk = -(-slot_count * 3 // 8 // 16) * 16
    cols = model_width // n_dp

    sent = stripe(jnp.concatenate([hidden_in, out_grad], axis=2), n_dp)
    fill_tile = jnp.broadcast_to(pack_fill, (micro, 128))
    gain_tile = jnp.broadcast_to(norm_gain[None, :], (8, width))
    slots, fills, gain_full = exchange(
        [sent, fill_tile, gain_tile],
        (("dp", "split"), ("dp", "all"), ("mp", "all")),
        0,
    )
    slots = slots.reshape(slot_count, 2 * width)
    fills = fills[:, :, 0].T
    gain_full = gain_full[:, 0, :].reshape(model_width)
    inv_count = 1.0 / jnp.sum(fills).astype(jnp.float32)

    odd = (jnp.arange(micro, dtype=jnp.int32) % 2)[None, :, None]
    steps = jnp.arange(share, dtype=jnp.int32)[None, None, :]
    start = jnp.where(odd == 1, n_dp - 1 - me, me)
    live = (start + steps * n_dp < fills.T[:, :, None]).reshape(slot_count)
    slot_ids = jnp.arange(slot_count, dtype=jnp.int32)
    before = (slot_ids[None, :] < slot_ids[:, None]) & live[None, :]
    place = jnp.where(live, jnp.sum(before.astype(jnp.int32), axis=1), -1)

    ranks = jnp.arange(n_dp, dtype=jnp.int32)[:, None, None]
    starts = jnp.where(odd.reshape(1, micro, 1) == 1, n_dp - 1 - ranks, ranks)
    counts = jnp.clip((fills[None] - starts + n_dp - 1) // n_dp, 0, share)
    most = jnp.max(jnp.sum(counts, axis=(1, 2)))
    chunk_total = (most + chunk - 1) // chunk

    def run_chunk(index):
        spots = jnp.arange(chunk, dtype=jnp.int32) + index * chunk
        pick = (spots[:, None] == place[None, :]).astype(jnp.bfloat16)
        packed = jnp.dot(pick, slots, preferred_element_type=jnp.float32)
        tok_rows = packed[:, :width].astype(jnp.bfloat16)
        scaled = (packed[:, width:] * inv_count).astype(jnp.bfloat16)
        (both,) = exchange(
            [jnp.concatenate([tok_rows, scaled], axis=1)], (("mp", "all"),), 1
        )
        both = both.transpose(1, 0, 2)
        tok_full = both[:, :, :width].reshape(chunk, model_width).astype(jnp.float32)
        scaled_full = both[:, :, width:].reshape(chunk, model_width)
        squares = jnp.sum(tok_full * tok_full, axis=1, keepdims=True)
        inv_rms = lax.rsqrt(squares / model_width + epsilon)
        normed_full = (tok_full * inv_rms * gain_full[None, :]).astype(jnp.bfloat16)
        pre_act = jnp.dot(normed_full, up_weight, preferred_element_type=jnp.float32)
        activated = gelu_tanh(pre_act).astype(jnp.bfloat16)
        grad_act = contract_cols(scaled_full, down_weight)
        grad_pre = jax.vjp(gelu_tanh, pre_act)[1](grad_act)[0].astype(jnp.bfloat16)

        by_cols = jnp.concatenate(
            [
                normed_full.reshape(chunk, n_dp, cols),
                scaled_full.reshape(chunk, n_dp, cols),
            ],
            axis=2,
        ).transpose(1, 0, 2)

        row_part = jnp.sum(grad_pre.astype(jnp.float32) * pre_act, axis=1, keepdims=True)
        partial = contract_cols(grad_pre, up_weight).astype(jnp.bfloat16)
        shares, row_parts = exchange(
            [
                partial.reshape(chunk, n_mp, width).transpose(1, 0, 2),
                jnp.broadcast_to(row_part / inv_rms, (chunk, 128)),
            ],
            (("mp", "split"), ("mp", "all")),
            2,
        )
        grad_normed = jnp.sum(shares.astype(jnp.float32), axis=0)
        row_dot = jnp.sum(row_parts, axis=0)[:, :1]
        values = tok_rows.astype(jnp.float32)
        cubed = inv_rms * inv_rms * inv_rms
        in_rows = (
            scaled.astype(jnp.float32)
            + norm_gain[None, :] * grad_normed * inv_rms
            - values * cubed * row_dot / model_width
        ).astype(jnp.bfloat16)
        gain_term = jnp.sum(grad_normed * values * inv_rms, axis=0)
        back = contract_rows(pick, in_rows).astype(jnp.bfloat16)
        act_all, pre_all, by_cols, back, gain_parts = exchange(
            [
                activated,
                grad_pre,
                by_cols,
                back.reshape(n_dp, micro * share, width),
                jnp.broadcast_to(gain_term[None, :], (8, width)),
            ],
            (("dp", "tree"), ("dp", "tree"), ("dp", "split"), ("dp", "split"), ("dp", "all")),
            3,
        )
        by_cols = by_cols.reshape(n_dp * chunk, 2 * cols)
        up_term = contract_rows(by_cols[:, :cols], pre_all.reshape(n_dp * chunk, ff_shard))
        down_term = contract_rows(act_all.reshape(n_dp * chunk, ff_shard), by_cols[:, cols:])
        return (back, up_term, down_term, jnp.sum(gain_parts[:, 0], axis=0))

    def add_chunk(index, total):
        return jax.tree.map(jnp.add, total, run_chunk(index))

    total = run_chunk(jnp.int32(0))
    back, up_grad, down_grad, gain_acc = lax.fori_loop(1, chunk_total, add_chunk, total)
    return (unstripe(back, micro), up_grad, down_grad, gain_acc)


def solution(mesh):
    in_specs = (
        P(None, "dp", "mp"),
        P(None, "dp", "mp"),
        P(None, "dp"),
        P("mp"),
        P(None, "mp"),
        P("mp", None),
    )
    out_specs = (P(None, "dp", "mp"), P("dp", "mp"), P("mp", "dp"), P("mp"))
    return jax.shard_map(
        on_device, mesh=mesh, in_specs=in_specs, out_specs=out_specs, check_vma=False
    )
```

profile of v0, /device:TPU:0, one launch (start us, length us, event | category | flops | bytes accessed | tf_op | source)
XLA Modules:
  0.0 228.1 jit_solution(17288973773275399459)
XLA Ops:
  0.7 0.1 broadcast_add_fusion
  0.7 0.1 iota_select_fusion
  0.8 1.3 broadcast_in_dim.54.refs_1_
  2.1 1.3 broadcast_in_dim.55.refs_2_
  3.4 1.1 constant_dynamic-update-slice_fusion.1
  4.5 1.1 constant_dynamic-update-slice_fusion
  5.5 0.1 slice_bitcast_fusion.2
  5.6 0.2 copy_bitcast_fusion
  5.8 1.0 pad_maximum_fusion.1.refs_0_
  6.8 30.0 %shard_map.93 = (bf16[8,32,1792]{2,1,0:T(8,128)(2,1)}, s32[8,2,128]{2,1,0:T(2,128)}, f32[4,8,896]{2,1,0:T(8,128)}) custom-call(bf16[8,32,1792]{2,1,0:T(8,128)(2,1)} %pad_maximum_fusion.1.refs_0_, s32[2,128]{1,0:T(2,128)} %broadcast_in_dim.54.refs_1_, f32[8,896]{1,0:T(8,128)} %broadcast_in_dim.55.refs_2_), custom_call_target="tpu_custom_call" | custom-call | tf_op jit(solution)/shard_map/pallas_call | solution.py:154
  36.8 1.3 slice_reduce_fusion.4
  38.8 0.1 copy.87
  38.9 0.2 fusion.73
  39.1 0.6 reduce_max.9
  40.4 0.1 copy.88
  40.5 0.1 broadcast_compare_fusion
  40.6 0.1 lt.57
  40.7 0.1 convert_reduce_fusion.2
  40.8 0.6 broadcast_select_fusion
  41.4 0.9 fusion.81
  42.4 0.6 copy.96
  43.0 0.1 mul.444
  43.1 1.5 fusion.68
  44.6 0.9 copy-done.10
  45.4 0.8 pad_maximum_fusion.3.refs_0_
  46.2 19.3 %shard_map.94 = bf16[4,96,1792]{2,1,0:T(8,128)(2,1)} custom-call(bf16[96,1792]{1,0:T(8,128)(2,1)} %pad_maximum_fusion.3.refs_0_), custom_call_target="tpu_custom_call" | custom-call | tf_op jit(solution)/shard_map/pallas_call | solution.py:154
  65.5 1.3 multiply_reduce_fusion.2
  66.9 2.7 %slice_convert_fusion.2 = (f32[96,4,896]{2,0,1:T(8,128)S(1)}, bf16[4,12,8,896]{3,2,1,0:T(8,128)(2,1)}, f32[4,12,8,896]{3,2,1,0:T(8,128)S(1)}, bf16[96,4,896]{2,0,1:T(8,128)(2,1)}) fusion(bf16[96,4,1792]{2,0,1:T(8,128)(2,1)} %bitcast.138), kind=kLoop, calls=%fused_computation.88 | loop fusion | flops 344064 | bytes 5505024 | tf_op jit(solution)/shard_map/convert_element_type | solution.py:213
  69.5 2.0 copy.89
  71.5 1.9 reshape.302
  73.4 0.0 copy-start.17
  73.4 1.8 fusion.38
  75.2 0.1 copy.104
  75.3 9.6 %fusion.85 = f32[96,1792]{1,0:T(8,128)} fusion(bf16[96,3584]{1,0:T(8,128)(2,1)S(1)} %bitcast.141, bf16[1792,3584]{1,0:T(8,128)(2,1)} %param.13), kind=kOutput, calls=%fused_computation.163 | convolution fusion | flops 1233125376 | bytes 14221312 | tf_op jit(solution)/shard_map/dot_general | solution.py:25
  84.9 0.4 copy.90
  85.2 0.5 reshape_reshape.3
  85.7 0.0 copy-start.12
  85.7 0.2 copy.94
  86.0 0.9 copy-done.12
  86.9 1.5 maximum_bitcast_fusion.1.refs_2_
  88.4 0.1 copy.103
  88.5 0.0 copy-done.14
  88.5 0.0 slice-start.1
  88.6 0.0 slice-start.2
  88.6 0.0 slice-start.3
  88.6 8.3 %multiply_reduce_fusion.3 = (f32[96]{0:T(128)S(1)}, bf16[96,1792]{1,0:T(8,128)(2,1)S(1)}, bf16[96,1792]{1,0:T(8,128)(2,1)}) fusion(f32[96,1792]{1,0:T(8,128)S(1)} %copy-done.14, bf16[3584,1792]{1,0:T(8,128)(2,1)} %param.12, f32[96,3584]{1,0:T(8,128)S(1)} %bitcast.136, f32[3584]{0:T(1024)S(1)} %mul.425, f32[96]{0:T(128)S(1)} %fusion.77), kind=kOutput, calls=%fused_computation.89 | convolution fusion | flops 1238458240 | bytes 15612672 | tf_op jit(solution)/shard_map/dot_general | solution.py:218
  96.9 0.7 broadcast_in_dim.57.refs_1_
  97.6 0.0 slice-done.1
  97.6 0.0 slice-done.3
  97.6 4.0 %convolution_convert_fusion.2 = bf16[96,3584]{1,0:T(8,128)(2,1)S(1)} fusion(bf16[96,1792]{1,0:T(8,128)(2,1)S(1)} %get-tuple-element.296.refs_1_, bf16[3584,1792]{1,0:T(8,128)(2,1)S(1)} %bitcast.122), kind=kOutput, calls=%fused_computation.63 | convolution fusion | flops 1233469440 | bytes 13877248 | tf_op jit(solution)/shard_map/dot_general | solution.py:25
  101.6 0.0 copy-done.13
  101.6 0.9 copy.122
  102.5 14.1 %shard_map.95 = (bf16[4,96,896]{2,1,0:T(8,128)(2,1)}, f32[4,96,128]{2,1,0:T(8,128)}) custom-call(bf16[4,96,896]{2,1,0:T(8,128)(2,1)} %bitcast.140, f32[96,128]{1,0:T(8,128)} %broadcast_in_dim.57.refs_1_), custom_call_target="tpu_custom_call" | custom-call | tf_op jit(solution)/shard_map/pallas_call | solution.py:154
  116.6 1.3 convert_reduce_fusion.1
  117.9 0.1 fusion.59
  118.0 0.6 broadcast_in_dim.58.refs_4_
  118.7 0.1 slice_reduce_fusion.2
  118.8 1.9 convolution_convert_fusion.3
  120.7 95.3 %shard_map.96 = (bf16[8,96,1792]{2,1,0:T(8,128)(2,1)}, bf16[8,96,1792]{2,1,0:T(8,128)(2,1)}, bf16[8,96,896]{2,1,0:T(8,128)(2,1)}, bf16[8,32,896]{2,1,0:T(8,128)(2,1)}, f32[8,8,896]{2,1,0:T(8,128)}) custom-call(bf16[96,1792]{1,0:T(8,128)(2,1)} %get-tuple-element.310.refs_0_, bf16[96,1792]{1,0:T(8,128)(2,1)} %copy-done.13, ...), custom_call_target="tpu_custom_call" | custom-call | tf_op jit(solution)/shard_map/pallas_call | solution.py:154
  216.0 1.6 slice_reduce_fusion.3
  217.5 5.4 %fusion.39 = f32[1792,448]{0,1:T(8,128)} fusion(bf16[768,1792]{1,0:T(8,128)(2,1)} %bitcast.150, bf16[768,896]{1,0:T(8,128)(2,1)} %bitcast.146), kind=kOutput, calls=%fused_computation.75 | convolution fusion | flops 1233125376 | bytes 6750208 | tf_op jit(solution)/shard_map/dot_general | solution.py:19
  222.9 3.1 %fusion.41 = f32[448,1792]{1,0:T(8,128)} fusion(bf16[768,1792]{1,0:T(8,128)(2,1)S(1)} %bitcast.139, bf16[768,896]{1,0:T(8,128)(2,1)S(1)} %bitcast.147), kind=kOutput, calls=%fused_computation.77 | convolution fusion | flops 1233125376 | bytes 6750208 | tf_op jit(solution)/shard_map/dot_general | solution.py:19
  226.1 1.1 slice_bitcast_fusion.3
  227.3 0.8 pad_maximum_fusion.2
  (33 shorter events, 0.3 us)
Async XLA Ops:
  44.5 0.9 copy-start.10
  73.4 1.8 copy-start.17
  75.3 9.6 %copy-start.16 = (bf16[96,4,896]{2,0,1:T(8,128)(2,1)S(1)}, bf16[96,4,896]{2,0,1:T(8,128)(2,1)}, u32[]{:S(2)}) copy-start(bf16[96,4,896]{2,0,1:T(8,128)(2,1)} %get-tuple-element.307) | copy-start | bytes 2064388
  85.7 1.1 copy-start.12
  86.9 1.7 copy-start.14
  88.4 9.2 %slice-start = ((s8[12845056]{0:T(1024)(128)(4,1)}), s8[4194304]{0:T(1024)(128)(4,1)S(1)}, s32[]{:S(2)}) async-start(s8[12845056]{0:T(1024)(128)(4,1)} %bitcast.121), calls=%async_computation | async-start | bytes 8388608
  88.5 9.1 %slice-start.1 = ((s8[12845056]{0:T(1024)(128)(4,1)}), s8[4194304]{0:T(1024)(128)(4,1)S(1)}, s32[]{:S(2)}) async-start(s8[12845056]{0:T(1024)(128)(4,1)} %bitcast.121), calls=%async_computation.1 | async-start | bytes 8388608
  88.6 9.0 %slice-start.2 = ((s8[12845056]{0:T(1024)(128)(4,1)}), s8[4194304]{0:T(1024)(128)(4,1)S(1)}, s32[]{:S(2)}) async-start(s8[12845056]{0:T(1024)(128)(4,1)} %bitcast.121), calls=%async_computation.2 | async-start | bytes 8388608
  88.6 9.0 %slice-start.3 = ((s8[12845056]{0:T(1024)(128)(4,1)}), s8[262144]{0:T(1024)(128)(4,1)S(1)}, s32[]{:S(2)}) async-start(s8[12845056]{0:T(1024)(128)(4,1)} %bitcast.121), calls=%async_computation.3 | async-start | bytes 524288
  96.8 4.7 %copy-start.13 = (bf16[96,1792]{1,0:T(8,128)(2,1)}, bf16[96,1792]{1,0:T(8,128)(2,1)S(1)}, u32[]{:S(2)}) copy-start(bf16[96,1792]{1,0:T(8,128)(2,1)S(1)} %get-tuple-element.296.refs_1_) | copy-start | bytes 1032196
  101.6 16.3 %copy-start.11 = (f32[96,1792]{1,0:T(8,128)S(1)}, f32[96,1792]{1,0:T(8,128)}, u32[]{:S(2)}) copy-start(f32[96,1792]{1,0:T(8,128)} %copy-done.10) | copy-start | bytes 2064388
  116.6 2.0 copy-start.19
  217.5 5.4 %copy-start.15 = (bf16[8,96,1792]{2,1,0:T(8,128)(2,1)S(1)}, bf16[8,96,1792]{2,1,0:T(8,128)(2,1)}, u32[]{:S(2)}) copy-start(bf16[8,96,1792]{2,1,0:T(8,128)(2,1)} %get-tuple-element.195) | copy-start | bytes 8257540
  217.5 5.4 %copy-start.18 = (bf16[8,96,896]{2,1,0:T(8,128)(2,1)S(1)}, bf16[8,96,896]{2,1,0:T(8,128)(2,1)}, u32[]{:S(2)}) copy-start(bf16[8,96,896]{2,1,0:T(8,128)(2,1)} %get-tuple-element.194) | copy-start | bytes 4128772
where the time goes:
time: 229 us; the launch traced here: 228 us
  Pallas kernels  159 us (69%)
  matrix products  33.7 us (15%)
  local copies, waits for them, and re-layouts  17.3 us (8%)
  other arithmetic  16 us (7%)
  between operations  2.34 us (1%)
    pallas_call x4, Pallas kernels, exchange(): pl.pallas_call(functools.partial(exchange_kernel, axes), out_shape=shapes...  159 us
    dot_general x2, matrix products, contract_cols(): lax.dot_general(left, right, (((1,), (1,)), ((), ())), preferred_element_...  13.5 us
    dot_general x3, matrix products, contract_rows(): lax.dot_general(left, right, (((0,), (0,)), ((), ())), preferred_element_...  10.4 us
    dot_general x1, matrix products, run_chunk(): jnp.dot(normed_full, up_weight, preferred_element_type=jnp.float32)  8.27 us

commit v1 on v0

--- a/solution.py
+++ b/solution.py
@@ -273,6 +273,455 @@
     return (unstripe(back, micro), up_grad, down_grad, gain_acc)
 
 
+gelu_slope = 0.7978845608028654
+gelu_cube = 0.044715
+MESH = pl.DeviceIdType.MESH
+
+
+def packed_chunk(slot_count):
+    return -(-slot_count * 3 // 8 // 16) * 16
+
+
+def fused_kernel(
+    hid, og, fill, gain, index, up_hbm, down_hbm,
+    in_part, up_out, down_out, gain_out, fills_out,
+    upw, dnw, hbuf, gbuf, act, pre, normed, nsl, gsl, gp_own,
+    sent_h, sent_g, got_h, got_g, fill_send, gain_send, gain_full,
+    part, shares, row_send, rows_in, term_send, terms_in,
+    sent_back, got_back, perm, pick,
+    w_sem, h0_s, h0_r, g0_s, g0_r, f_s, f_r, n_s, n_r,
+    ht_s, ht_r, gt_s, gt_r, p_s, p_r, q_s, q_r, b_s, b_r, t_s, t_r,
+):
+    n_dp, n_mp = lax.axis_size("dp"), lax.axis_size("mp")
+    me, mine = lax.axis_index("dp"), lax.axis_index("mp")
+    core = lax.rem(mine, 2)
+    high = lax.div(mine, 2)
+    low = lax.rem(me, 2)
+    micro, tok, width = hid.shape
+    model, ff = upw.shape
+    rows = micro * tok
+    share = tok // n_dp
+    per = micro * share
+    chunk = hbuf.shape[0] // n_dp
+    cols = model // n_dp
+    group = 2 * chunk
+    tile = 256
+    f32, bf16 = jnp.float32, jnp.bfloat16
+
+    loads = [
+        pltpu.make_async_copy(up_hbm, upw, w_sem.at[0]),
+        pltpu.make_async_copy(down_hbm, dnw, w_sem.at[1]),
+    ]
+    for load in loads:
+        load.start()
+
+    barrier = pltpu.get_barrier_semaphore()
+    for axis, n, at in (("dp", n_dp, me), ("mp", n_mp, mine)):
+        for d in range(1, n):
+            pl.semaphore_signal(
+                barrier, inc=1, device_id={axis: lax.rem(at + d, n)}, device_id_type=MESH
+            )
+
+    shift = share.bit_length() - 1
+    line = lax.broadcasted_iota(jnp.int32, (rows, rows), 0)
+    lane = lax.broadcasted_iota(jnp.int32, (rows, rows), 1)
+    m_of = (line >> shift) & (micro - 1)
+    d_of = line >> (per.bit_length() - 1)
+    first = jnp.where((m_of & 1) == 1, n_dp - 1 - d_of, d_of)
+    source = m_of * tok + (line & (share - 1)) * n_dp + first
+    perm[...] = (source == lane).astype(f32).astype(bf16)
+    for block, target in ((hid, sent_h), (og, sent_g)):
+        for m in range(micro):
+            piece = jnp.dot(
+                perm[:, m * tok : (m + 1) * tok], block[m], preferred_element_type=f32
+            )
+            if m == 0:
+                total = piece
+            else:
+                total = total + piece
+        target[...] = total.astype(bf16)
+    ids = lax.broadcasted_iota(jnp.int32, fill_send.shape, 0)
+    tile_fill = jnp.zeros(fill_send.shape, jnp.int32)
+    for m in range(micro):
+        tile_fill = jnp.where(ids == m, fill[m, 0], tile_fill)
+    fill_send[...] = tile_fill
+    gain_send[...] = jnp.broadcast_to(gain[...], gain_send.shape)
+
+    pl.semaphore_wait(barrier, n_dp + n_mp - 2)
+
+    sent = []
+
+    def ship(src, dst, s_sem, r_sem, device):
+        copy = pltpu.make_async_remote_copy(
+            src_ref=src, dst_ref=dst, send_sem=s_sem, recv_sem=r_sem,
+            device_id=device, device_id_type=MESH,
+        )
+        copy.start()
+        sent.append(copy)
+        return copy
+
+    def to_dp(source_of, target, s_sems, r_sems):
+        out = []
+        for d in [n_dp // 2] + [d for d in range(1, n_dp) if d != n_dp // 2]:
+            peer = lax.rem(me + d, n_dp)
+            out.append(ship(source_of(peer), target, s_sems.at[d], r_sems.at[d], {"dp": peer}))
+        return out
+
+    def to_mp(source_of, target, s_sems, r_sems):
+        out = []
+        for d in range(1, n_mp):
+            peer = lax.rem(mine + d, n_mp)
+            out.append(ship(source_of(peer), target, s_sems.at[d], r_sems.at[d], {"mp": peer}))
+        return out
+
+    def slot(ref, r):
+        return ref.at[pl.ds(pl.multiple_of(r * per, per), per), :]
+
+    def strip(q):
+        return pl.ds(pl.multiple_of(q * width, 128), width)
+
+    def rank_rows(r):
+        return pl.ds(pl.multiple_of(r * chunk, 16), chunk)
+
+    fill_copies = to_dp(lambda peer: fill_send, fills_out.at[me], f_s, f_r)
+    h_copies = to_dp(lambda peer: slot(sent_h, peer), slot(got_h, me), h0_s, h0_r)
+    gain_copies = to_mp(lambda peer: gain_send, gain_full.at[:, strip(mine)], n_s, n_r)
+    g_copies = to_dp(lambda peer: slot(sent_g, peer), slot(got_g, me), g0_s, g0_r)
+    here = pl.ds(pl.multiple_of(me * per, per), per)
+    got_h[here, :] = sent_h[here, :]
+    got_g[here, :] = sent_g[here, :]
+    fills_out[me] = fill_send[...]
+    gain_full[:, strip(mine)] = gain_send[...]
+
+    for copy in fill_copies:
+        copy.wait_recv()
+    lanes = lax.broadcasted_iota(jnp.int32, (1, rows), 1)
+    count = jnp.zeros((1, rows), jnp.int32)
+    token_total = jnp.zeros((1, 1), jnp.int32)
+    for r in range(n_dp):
+        for m in range(micro):
+            one = fills_out[r, m : m + 1, 0:1]
+            token_total = token_total + one
+            count = jnp.where((lanes >> shift) == r * micro + m, one, count)
+    odd = (lanes >> shift) & 1
+    begin = jnp.where(odd == 1, n_dp - 1 - me, me)
+    live = begin + (lanes & (share - 1)) * n_dp < count
+    inv_count = 1.0 / token_total.astype(f32)
+    live_f = live.astype(f32)
+    upto = (line < lane).astype(f32).astype(bf16)
+    place = jnp.dot(
+        jnp.broadcast_to(live_f, (16, rows)).astype(bf16), upto, preferred_element_type=f32
+    )[0:1, :]
+    place = jnp.where(live, place, -1.0)
+    spots = (lax.broadcasted_iota(jnp.int32, (chunk, rows), 0) + index[0] * chunk).astype(f32)
+    pick[...] = (spots == place).astype(f32).astype(bf16)
+
+    def along(at_dp, at_mp, x, y):
+        return (
+            at_dp + x - 2 * x * lax.rem(at_dp, 2),
+            at_mp + 2 * y - 4 * y * lax.div(at_mp, 2),
+        )
+
+    def owner(t, at_mp, c):
+        t1, t0 = (t >> 1) & 1, t & 1
+        x = t1 * (1 - c) + t0 * c
+        y = t0 * (1 - c) + t1 * c
+        return along(flipped_by(me, (t >> 2) * 2), at_mp, x, y)
+
+    def toward(bit):
+        if bit >= 4:
+            return flipped(me, bit // 2), mine
+        if bit == 2:
+            return along(me, mine, 1 - core, core)
+        return along(me, mine, core, 1 - core)
+
+    nodes = 2 * n_dp
+    top = n_dp
+    partner = mine + 1 - 2 * core
+    trees = {"h": (hbuf, ht_s, ht_r), "g": (gbuf, gt_s, gt_r)}
+    tree_copies = {}
+
+    def forward(k, t):
+        buf, s_sems, r_sems = trees[k]
+        dp_o, mp_o = owner(t, mine, core)
+        place_ = buf.at[rank_rows(dp_o), strip(mp_o)]
+        bit = (t & -t) // 2 if t else top
+        while bit >= 1:
+            dp_t, mp_t = toward(bit)
+            tree_copies[k, t ^ bit] = ship(
+                place_, place_, s_sems.at[t ^ bit], r_sems.at[t ^ bit], {"dp": dp_t, "mp": mp_t}
+            )
+            bit //= 2
+        tree_copies[k, nodes + t] = ship(
+            place_, place_, s_sems.at[nodes + t], r_sems.at[nodes + t], {"mp": partner}
+        )
+
+    def arrive(k, *ts):
+        for t in ts:
+            tree_copies[k, t].wait_recv()
+            forward(k, t)
+
+    def joined(k, z):
+        for t in range(4 * z, 4 * z + 4):
+            tree_copies[k, nodes + t].wait_recv()
+
+    def base_of(z):
+        return 2 * flipped_by(lax.div(me, 2), z)
+
+    half = lax.div(me, n_dp // n_mp)
+    part_at = lax.rem(me, n_dp // n_mp)
+
+    def slice_cols(value):
+        out = value[:, 0:cols]
+        for i in range(1, n_dp // n_mp):
+            out = jnp.where(part_at == i, value[:, i * cols : (i + 1) * cols], out)
+        return out
+
+    def rms(block):
+        return lax.rsqrt(jnp.sum(block * block, axis=1, keepdims=True) / model + epsilon)
+
+    def do_pre(z):
+        joined("h", z)
+        base = base_of(z)
+
+        def norm_rows(i, carry):
+            src = pl.ds(pl.multiple_of(base * chunk + i * 16, 16), 16)
+            dst = pl.ds(pl.multiple_of(i * 16, 16), 16)
+            value = hbuf[src, :].astype(f32)
+            normed[dst, :] = (value * rms(value) * gain_full[0:1, :]).astype(bf16)
+            return carry
+
+        lax.fori_loop(0, group // 16, norm_rows, 0)
+        nsl[z] = slice_cols(normed[:, strip(half)].astype(f32)).astype(bf16)
+
+        def pre_tile(n, carry):
+            at = pl.ds(pl.multiple_of(n * tile, tile), tile)
+            value = jnp.dot(normed[...], upw[:, at], preferred_element_type=f32)
+            pre[z, :, at] = value
+            bent = jnp.tanh(gelu_slope * (value + gelu_cube * (value * value * value)))
+            act[z, :, at] = (value * (0.5 * (1.0 + bent))).astype(bf16)
+            return carry
+
+        lax.fori_loop(0, ff // tile, pre_tile, 0)
+
+    def do_grad(z):
+        joined("g", z)
+        base = base_of(z)
+        block = pl.ds(pl.multiple_of(base * chunk, 16), group)
+        gsl[...] = slice_cols(gbuf[block, strip(half)].astype(f32)).astype(bf16)
+
+        def grad_tile(n, carry):
+            at = pl.ds(pl.multiple_of(n * tile, tile), tile)
+            grad = contract_cols(gbuf[block, :], dnw[at, :])
+            value = pre[z, :, at]
+            square = value * value
+            bent = jnp.tanh(gelu_slope * (value + gelu_cube * (square * value)))
+            slope = 0.5 * (1.0 + bent) + (0.5 * value) * (1.0 - bent * bent) * (
+                gelu_slope * (1.0 + 3.0 * gelu_cube * square)
+            )
+            back = (grad * slope).astype(bf16)
+            if z == 0:
+                gp_own[:, at] = back
+            up_term = contract_rows(nsl[z], back)
+            down_term = contract_rows(act[z, :, at], gsl[...])
+            if z == 0:
+                up_out[:, at] = up_term
+                down_out[at, :] = down_term
+            else:
+                up_out[:, at] += up_term
+                down_out[at, :] += down_term
+            return carry
+
+        lax.fori_loop(0, ff // tile, grad_tile, 0)
+
+    def compact(got, buf, scale):
+        packed = jnp.dot(pick[...], got[...], preferred_element_type=f32)
+        if scale is not None:
+            packed = packed * scale
+        buf[rank_rows(me), strip(mine)] = packed.astype(bf16)
+
+    for copy in h_copies:
+        copy.wait_recv()
+    compact(got_h, hbuf, None)
+    forward("h", 0)
+    for copy in gain_copies:
+        copy.wait_recv()
+    arrive("h", 8, 4, 2, 1)
+    for copy in g_copies:
+        copy.wait_recv()
+    compact(got_g, gbuf, inv_count)
+    forward("g", 0)
+    arrive("h", 12, 3, 6, 10)
+    loads[0].wait()
+    do_pre(0)
+    arrive("h", 14, 5, 7)
+    arrive("g", 8, 4)
+    do_pre(1)
+    arrive("h", 9, 11)
+    arrive("g", 2, 1)
+    do_pre(2)
+    arrive("h", 13, 15)
+    arrive("g", 12)
+    do_pre(3)
+    arrive("g", 3, 6, 10)
+    loads[1].wait()
+    do_grad(0)
+
+    own = pl.ds(pl.multiple_of(low * chunk, 16), chunk)
+    own_gp = gp_own[own, :]
+    own_pre = pre[0, own, :]
+    inv_rms = rms(hbuf[rank_rows(me), :].astype(f32))
+    row_part = jnp.sum(own_gp.astype(f32) * own_pre, axis=1, keepdims=True)
+    row_send[...] = jnp.broadcast_to(row_part / inv_rms, row_send.shape)
+
+    def part_tile(n, carry):
+        at = pl.ds(pl.multiple_of(n * tile, tile), tile)
+        part[:, at] = contract_cols(gp_own[own, :], upw[at, :]).astype(bf16)
+        return carry
+
+    lax.fori_loop(0, model // tile, part_tile, 0)
+    part_copies = to_mp(lambda peer: part.at[:, strip(peer)], shares.at[mine], p_s, p_r)
+    part_copies += to_mp(lambda peer: row_send, rows_in.at[mine], q_s, q_r)
+
+    arrive("g", 14, 5, 7)
+    do_grad(1)
+
+    for copy in part_copies:
+        copy.wait_recv()
+    grad_normed = part[:, strip(mine)].astype(f32)
+    row_dot = row_send[:, 0:1]
+    for d in range(1, n_mp):
+        peer = lax.rem(mine + d, n_mp)
+        grad_normed = grad_normed + shares[peer].astype(f32)
+        row_dot = row_dot + rows_in[peer][:, 0:1]
+    values = hbuf[rank_rows(me), strip(mine)].astype(f32)
+    scaled = gbuf[rank_rows(me), strip(mine)].astype(f32)
+    cubed = inv_rms * inv_rms * inv_rms
+    in_rows = (
+        scaled + gain[...] * grad_normed * inv_rms - values * (cubed * row_dot / model)
+    ).astype(bf16)
+    gain_term = jnp.sum(grad_normed * values * inv_rms, axis=0, keepdims=True)
+    term_send[...] = jnp.broadcast_to(gain_term, term_send.shape)
+    terms_in[me] = term_send[...]
+    back = contract_rows(pick[...], in_rows).astype(bf16)
+    sent_back[...] = back
+    got_back[here, :] = sent_back[here, :]
+    back_copies = to_dp(lambda peer: slot(sent_back, peer), slot(got_back, me), b_s, b_r)
+    back_copies += to_dp(lambda peer: term_send, terms_in.at[me], t_s, t_r)
+
+    arrive("g", 9, 11)
+    do_grad(2)
+    arrive("g", 13, 15)
+    do_grad(3)
+
+    for copy in back_copies:
+        copy.wait_recv()
+    gain_out[...] = jnp.sum(terms_in[...], axis=0)
+    for m in range(micro):
+        in_part[m] = contract_rows(perm[:, m * tok : (m + 1) * tok], got_back[...]).astype(bf16)
+    for copy in sent:
+        copy.wait_send()
+
+
+def fused_call(hidden_in, out_grad, pack_fill, norm_gain, index, up_weight, down_weight):
+    micro, tok, width = hidden_in.shape
+    model, ff = up_weight.shape
+    n_dp, n_mp = lax.axis_size("dp"), lax.axis_size("mp")
+    rows = micro * tok
+    per = rows // n_dp
+    chunk = packed_chunk(rows)
+    cols = model // n_dp
+    group = 2 * chunk
+    zs = n_dp // 2
+    f32, bf16 = jnp.float32, jnp.bfloat16
+    vmem = pl.BlockSpec(memory_space=pltpu.VMEM)
+    smem = pl.BlockSpec(memory_space=pltpu.SMEM)
+    hbm = pl.BlockSpec(memory_space=pl.ANY)
+    dma = pltpu.SemaphoreType.DMA
+    return pl.pallas_call(
+        fused_kernel,
+        out_shape=[
+            jax.ShapeDtypeStruct((micro, tok, width), bf16),
+            jax.ShapeDtypeStruct((cols, ff), f32),
+            jax.ShapeDtypeStruct((ff, cols), f32),
+            jax.ShapeDtypeStruct((8, width), f32),
+            jax.ShapeDtypeStruct((n_dp, 8, 128), jnp.int32),
+        ],
+        in_specs=[vmem, vmem, smem, vmem, smem, hbm, hbm],
+        out_specs=[vmem] * 5,
+        scratch_shapes=[
+            pltpu.VMEM((model, ff), bf16),
+            pltpu.VMEM((ff, model), bf16),
+            pltpu.VMEM((n_dp * chunk, model), bf16),
+            pltpu.VMEM((n_dp * chunk, model), bf16),
+            pltpu.VMEM((zs, group, ff), bf16),
+            pltpu.VMEM((zs, group, ff), f32),
+            pltpu.VMEM((group, model), bf16),
+            pltpu.VMEM((zs, group, cols), bf16),
+            pltpu.VMEM((group, cols), bf16),
+            pltpu.VMEM((group, ff), bf16),
+            pltpu.VMEM((rows, width), bf16),
+            pltpu.VMEM((rows, width), bf16),
+            pltpu.VMEM((rows, width), bf16),
+            pltpu.VMEM((rows, width), bf16),
+            pltpu.VMEM((8, 128), jnp.int32),
+            pltpu.VMEM((8, width), f32),
+            pltpu.VMEM((8, model), f32),
+            pltpu.VMEM((chunk, model), bf16),
+            pltpu.VMEM((n_mp, chunk, width), bf16),
+            pltpu.VMEM((chunk, 128), f32),
+            pltpu.VMEM((n_mp, chunk, 128), f32),
+            pltpu.VMEM((8, width), f32),
+            pltpu.VMEM((n_dp, 8, width), f32),
+            pltpu.VMEM((rows, width), bf16),
+            pltpu.VMEM((rows, width), bf16),
+            pltpu.VMEM((rows, rows), bf16),
+            pltpu.VMEM((chunk, rows), bf16),
+            dma((2,)),
+        ]
+        + [dma((n_dp,))] * 6
+        + [dma((n_mp,))] * 2
+        + [dma((4 * n_dp,))] * 4
+        + [dma((n_mp,))] * 4
+        + [dma((n_dp,))] * 4,
+        compiler_params=pltpu.CompilerParams(
+            collective_id=7, has_side_effects=True, vmem_limit_bytes=67043328
+        ),
+        cost_estimate=pl.CostEstimate(
+            flops=8 * rows * model * ff, bytes_accessed=6 * model * ff, transcendentals=0
+        ),
+    )(hidden_in, out_grad, pack_fill, norm_gain[None, :], index, up_weight, down_weight)
+
+
+def on_device_fused(hidden_in, out_grad, pack_fill, norm_gain, up_weight, down_weight):
+    micro, tok, _ = hidden_in.shape
+    n_dp = lax.axis_size("dp")
+    share = tok // n_dp
+    chunk = packed_chunk(micro * tok)
+
+    def run_chunk(index):
+        return fused_call(
+            hidden_in, out_grad, pack_fill, norm_gain,
+            jnp.reshape(index, (1,)).astype(jnp.int32), up_weight, down_weight,
+        )
+
+    *total, fills = run_chunk(jnp.int32(0))
+    fills = fills[:, :micro, 0].T
+    odd = (jnp.arange(micro, dtype=jnp.int32) % 2).reshape(1, micro, 1)
+    ranks = jnp.arange(n_dp, dtype=jnp.int32)[:, None, None]
+    starts = jnp.where(odd == 1, n_dp - 1 - ranks, ranks)
+    counts = jnp.clip((fills[None] - starts + n_dp - 1) // n_dp, 0, share)
+    most = jnp.max(jnp.sum(counts, axis=(1, 2)))
+    chunk_total = (most + chunk - 1) // chunk
+
+    def add_chunk(index, so_far):
+        *more, _ = run_chunk(index)
+        return jax.tree.map(jnp.add, so_far, more)
+
+    in_grad, up_grad, down_grad, gain = lax.fori_loop(1, chunk_total, add_chunk, total)
+    return (in_grad, up_grad, down_grad, gain[0])
+
+
 def solution(mesh):
     in_specs = (
         P(None, "dp", "mp"),
@@ -283,6 +732,22 @@
         P("mp", None),
     )
     out_specs = (P(None, "dp", "mp"), P("dp", "mp"), P("mp", "dp"), P("mp"))
+
+    def local(hidden_in, out_grad, pack_fill, norm_gain, up_weight, down_weight):
+        micro, tok, width = hidden_in.shape
+        n_dp, n_mp = mesh.shape["dp"], mesh.shape["mp"]
+        share = tok // n_dp
+        fits = (
+            (n_dp, n_mp, micro) == (8, 4, 2)
+            and width % 128 == 0
+            and up_weight.shape[1] % 256 == 0
+            and up_weight.shape[0] % 256 == 0
+            and tok % 128 == 0
+            and share & (share - 1) == 0
+        )
+        body = on_device_fused if fits else on_device
+        return body(hidden_in, out_grad, pack_fill, norm_gain, up_weight, down_weight)
+
     return jax.shard_map(
-        on_device, mesh=mesh, in_specs=in_specs, out_specs=out_specs, check_vma=False
+        local, mesh=mesh, in_specs=in_specs, out_specs=out_specs, check_vma=False
     )

time: 229 us -> 152 us (0.66)
  matrix products: 33.7 us -> 0 us
  Pallas kernels: 159 us -> 133 us
  other arithmetic: 16 us -> 2.15 us
  local copies, waits for them, and re-layouts: 17.3 us -> 14.7 us
    dot_general x7 -> x0, matrix products: 33.7 us -> none  [the longest x2 13.5 us: contract_cols(): lax.dot_general(left, right, (((1,), (1,)), ((), ())), preferred_element_...]
    pallas_call x4 -> x1, Pallas kernels: 159 us -> 133 us  [fused_call(): pl.pallas_call(fused_kernel, out_shape=[jax.ShapeDtypeStruct((micro, tok,...]
    unnamed x29 -> x6, local copies, waits for them, and re-layouts: 2.85 us -> 9.99 us
    reduce_sum x8 -> x1, other arithmetic: 5.95 us -> 0.87 us  [on_device_fused(): most = jnp.max(jnp.sum(counts, axis=(1, 2)))]
    convert_element_type x3 -> x0, other arithmetic: 4.49 us -> none  [the longest x1 2.68 us: run_chunk(): both[:, :, :width].reshape(chunk, model_width).astype(jnp.float32)]
    convert_element_type x3 -> x0, local copies, waits for them, and re-layouts: 4.02 us -> none  [run_chunk(): both[:, :, :width].reshape(chunk, model_width).astype(jnp.float32)]
where the time goes in v1:
time: 152 us
  Pallas kernels  133 us (88%)
  local copies, waits for them, and re-layouts  14.7 us (10%)
  other arithmetic  2.15 us (1%)
    pallas_call x1, Pallas kernels, fused_call(): pl.pallas_call(fused_kernel, out_shape=[jax.ShapeDtypeStruct((micro, tok,...  133 us
    unnamed x6, local copies, waits for them, and re-layouts  9.99 us

profile of v1, /device:TPU:0, one launch (start us, length us, event | category | flops | bytes accessed | tf_op | source)
XLA Modules:
  0.0 151.5 jit_solution(7726268621728037798)
XLA Ops:
  0.7 0.6 iota_select_fusion
  1.3 1.3 copy.14.fill
  2.6 1.3 broadcast_in_dim.39
  3.9 1.3 broadcast_in_dim.32.gain
  5.1 133.1 %shard_map.93 = (bf16[2,128,896]{2,1,0:T(8,128)(2,1)}, f32[448,1792]{1,0:T(8,128)}, f32[1792,448]{1,0:T(8,128)}, f32[8,896]{1,0:T(8,128)}, s32[8,8,128]{2,1,0:T(8,128)}) custom-call(bf16[2,128,896]{2,1,0:T(8,128)(2,1)} %hid.1, bf16[2,128,896]{2,1,0:T(8,128)(2,1)} %og.1, s32[2,1]{1,0:T(2,128)} %copy.14.fill, f32[1,896]{1,0:T(1,128)} %broadcast_in_dim.32.gain, ...), custom_call_target="tpu_custom_call" | custom-call | flops 13153337344 | bytes 38535168 | tf_op jit(solution)/shard_map/pallas_call | solution.py:641
  138.2 0.8 slice.6
  139.0 0.1 copy.15
  139.1 0.9 fusion.2
  140.0 0.6 reduce_max.9
  141.3 0.2 while.17
  141.5 1.4 slice_reduce_fusion
  142.8 0.0 copy-start.2
  142.8 5.2 %copy.17 = f32[1792,448]{0,1:T(8,128)} copy(f32[1792,448]{1,0:T(8,128)} %get-tuple-element.118) | data formatting | bytes 6422528
  148.0 1.8 %copy.35 = bf16[2,128,896]{2,1,0:T(8,128)(2,1)} copy(bf16[2,128,896]{2,1,0:T(8,128)(2,1)} %get-tuple-element.331) | data formatting | bytes 917504
  149.8 0.0 copy-done.2
  149.8 1.7 %copy.36 = f32[448,1792]{1,0:T(8,128)} copy(f32[448,1792]{1,0:T(8,128)S(1)} %copy-done.2) | data formatting | bytes 6422528
  (2 shorter events, 0.0 us)
Async XLA Ops:
  142.8 7.0 %copy-start.2 = (f32[448,1792]{1,0:T(8,128)S(1)}, f32[448,1792]{1,0:T(8,128)}, u32[]{:S(2)}) copy-start(f32[448,1792]{1,0:T(8,128)} %get-tuple-element.332) | copy-start | bytes 9633796

commit v2 on v1

--- a/solution.py
+++ b/solution.py
@@ -1,3 +1,4 @@
+import contextlib
 import functools
 
 import jax
@@ -273,6 +274,10 @@
     return (unstripe(back, micro), up_grad, down_grad, gain_acc)
 
 
+def phase(name):
+    return contextlib.nullcontext()
+
+
 gelu_slope = 0.7978845608028654
 gelu_cube = 0.044715
 MESH = pl.DeviceIdType.MESH
@@ -282,14 +287,26 @@
     return -(-slot_count * 3 // 8 // 16) * 16
 
 
+def dealing(micro, tok, n_dp):
+    rows, share = micro * tok, tok // n_dp
+    shift = share.bit_length() - 1
+    line = lax.broadcasted_iota(jnp.int32, (rows, rows), 0)
+    lane = lax.broadcasted_iota(jnp.int32, (rows, rows), 1)
+    m_of = (line >> shift) & (micro - 1)
+    d_of = line >> ((micro * share).bit_length() - 1)
+    first = jnp.where((m_of & 1) == 1, n_dp - 1 - d_of, d_of)
+    source = m_of * tok + (line & (share - 1)) * n_dp + first
+    return (source == lane).astype(jnp.float32).astype(jnp.bfloat16)
+
+
 def fused_kernel(
     hid, og, fill, gain, index, up_hbm, down_hbm,
-    in_part, up_out, down_out, gain_out, fills_out,
-    upw, dnw, hbuf, gbuf, act, pre, normed, nsl, gsl, gp_own,
-    sent_h, sent_g, got_h, got_g, fill_send, gain_send, gain_full,
+    act_o, gp_o, ns_o, gs_o, back_o, terms_o, trips,
+    upw, dnt, hbuf, gbuf, act, pre, normed, ns, gs, gp,
+    sent_h, sent_g, got_h, got_g, fills_out, fill_send, gain_send, gain_full,
     part, shares, row_send, rows_in, term_send, terms_in,
     sent_back, got_back, perm, pick,
-    w_sem, h0_s, h0_r, g0_s, g0_r, f_s, f_r, n_s, n_r,
+    w_sem, o_sem, h0_s, h0_r, g0_s, g0_r, f_s, f_r, n_s, n_r,
     ht_s, ht_r, gt_s, gt_r, p_s, p_r, q_s, q_r, b_s, b_r, t_s, t_r,
 ):
     n_dp, n_mp = lax.axis_size("dp"), lax.axis_size("mp")
@@ -305,15 +322,24 @@
     chunk = hbuf.shape[0] // n_dp
     cols = model // n_dp
     group = 2 * chunk
+    zs = n_dp // 2
     tile = 256
     f32, bf16 = jnp.float32, jnp.bfloat16
 
-    loads = [
-        pltpu.make_async_copy(up_hbm, upw, w_sem.at[0]),
-        pltpu.make_async_copy(down_hbm, dnw, w_sem.at[1]),
+    up_load = pltpu.make_async_copy(up_hbm, upw, w_sem.at[0])
+    up_load.start()
+    span = model // 2
+    slots = zs * group // tile
+    flips = [
+        pltpu.make_async_copy(
+            down_hbm.at[(i // 2) * tile : (i // 2 + 1) * tile, (i % 2) * span : (i % 2 + 1) * span],
+            act.at[(i % slots) * tile : (i % slots + 1) * tile, 0:span],
+            w_sem.at[1 + i % slots],
+        )
+        for i in range(2 * ff // tile)
     ]
-    for load in loads:
-        load.start()
+    for flip in flips[:slots]:
+        flip.start()
 
     barrier = pltpu.get_barrier_semaphore()
     for axis, n, at in (("dp", n_dp, me), ("mp", n_mp, mine)):
@@ -323,56 +349,55 @@
             )
 
     shift = share.bit_length() - 1
-    line = lax.broadcasted_iota(jnp.int32, (rows, rows), 0)
-    lane = lax.broadcasted_iota(jnp.int32, (rows, rows), 1)
-    m_of = (line >> shift) & (micro - 1)
-    d_of = line >> (per.bit_length() - 1)
-    first = jnp.where((m_of & 1) == 1, n_dp - 1 - d_of, d_of)
-    source = m_of * tok + (line & (share - 1)) * n_dp + first
-    perm[...] = (source == lane).astype(f32).astype(bf16)
-    for block, target in ((hid, sent_h), (og, sent_g)):
+    perm[...] = dealing(micro, tok, n_dp)
+
+    def deal(block, target):
+        total = 0.0
         for m in range(micro):
-            piece = jnp.dot(
+            total = total + jnp.dot(
                 perm[:, m * tok : (m + 1) * tok], block[m], preferred_element_type=f32
             )
-            if m == 0:
-                total = piece
-            else:
-                total = total + piece
         target[...] = total.astype(bf16)
+
+    deal(hid, sent_h)
     ids = lax.broadcasted_iota(jnp.int32, fill_send.shape, 0)
     tile_fill = jnp.zeros(fill_send.shape, jnp.int32)
     for m in range(micro):
-        tile_fill = jnp.where(ids == m, fill[m, 0], tile_fill)
+        tile_fill = jnp.where(ids == m, fill[0, m], tile_fill)
     fill_send[...] = tile_fill
-    gain_send[...] = jnp.broadcast_to(gain[...], gain_send.shape)
-
-    pl.semaphore_wait(barrier, n_dp + n_mp - 2)
-
-    sent = []
-
-    def ship(src, dst, s_sem, r_sem, device):
-        copy = pltpu.make_async_remote_copy(
+    gain_row = gain[...].reshape(1, width)
+    gain_send[...] = jnp.broadcast_to(gain_row, gain_send.shape)
+
+    with phase("barrier"):
+        pl.semaphore_wait(barrier, n_dp + n_mp - 2)
+
+    def remote(src, dst, s_sem, r_sem, device):
+        return pltpu.make_async_remote_copy(
             src_ref=src, dst_ref=dst, send_sem=s_sem, recv_sem=r_sem,
             device_id=device, device_id_type=MESH,
         )
-        copy.start()
-        sent.append(copy)
-        return copy
 
     def to_dp(source_of, target, s_sems, r_sems):
         out = []
         for d in [n_dp // 2] + [d for d in range(1, n_dp) if d != n_dp // 2]:
             peer = lax.rem(me + d, n_dp)
-            out.append(ship(source_of(peer), target, s_sems.at[d], r_sems.at[d], {"dp": peer}))
+            out.append(remote(source_of(peer), target, s_sems.at[d], r_sems.at[d], {"dp": peer}))
         return out
 
     def to_mp(source_of, target, s_sems, r_sems):
         out = []
         for d in range(1, n_mp):
             peer = lax.rem(mine + d, n_mp)
-            out.append(ship(source_of(peer), target, s_sems.at[d], r_sems.at[d], {"mp": peer}))
+            out.append(remote(source_of(peer), target, s_sems.at[d], r_sems.at[d], {"mp": peer}))
         return out
+
+    def start(copies):
+        for copy in copies:
+            copy.start()
+
+    def received(copies):
+        for copy in copies:
+            copy.wait_recv()
 
     def slot(ref, r):
         return ref.at[pl.ds(pl.multiple_of(r * per, per), per), :]
@@ -387,14 +412,33 @@
     h_copies = to_dp(lambda peer: slot(sent_h, peer), slot(got_h, me), h0_s, h0_r)
     gain_copies = to_mp(lambda peer: gain_send, gain_full.at[:, strip(mine)], n_s, n_r)
     g_copies = to_dp(lambda peer: slot(sent_g, peer), slot(got_g, me), g0_s, g0_r)
+    part_copies = to_mp(lambda peer: part.at[:, strip(peer)], shares.at[mine], p_s, p_r)
+    part_copies += to_mp(lambda peer: row_send, rows_in.at[mine], q_s, q_r)
+    back_copies = to_dp(lambda peer: slot(sent_back, peer), slot(got_back, me), b_s, b_r)
+    back_copies += to_dp(lambda peer: term_send, terms_in.at[me], t_s, t_r)
+    start(fill_copies)
+    start(h_copies)
+    start(gain_copies)
     here = pl.ds(pl.multiple_of(me * per, per), per)
     got_h[here, :] = sent_h[here, :]
-    got_g[here, :] = sent_g[here, :]
     fills_out[me] = fill_send[...]
     gain_full[:, strip(mine)] = gain_send[...]
 
-    for copy in fill_copies:
-        copy.wait_recv()
+    deal(og, sent_g)
+
+    with phase("flips"):
+        for i, flip in enumerate(flips):
+            flip.wait()
+            held = slice((i % slots) * tile, (i % slots + 1) * tile)
+            for j in range(span // tile):
+                to = slice((i % 2) * span + j * tile, (i % 2) * span + (j + 1) * tile)
+                dnt[to, (i // 2) * tile : (i // 2 + 1) * tile] = act[
+                    held, j * tile : (j + 1) * tile
+                ].T
+            if i + slots < len(flips):
+                flips[i + slots].start()
+    with phase("fills"):
+        received(fill_copies)
     lanes = lax.broadcasted_iota(jnp.int32, (1, rows), 1)
     count = jnp.zeros((1, rows), jnp.int32)
     token_total = jnp.zeros((1, 1), jnp.int32)
@@ -407,7 +451,21 @@
     begin = jnp.where(odd == 1, n_dp - 1 - me, me)
     live = begin + (lanes & (share - 1)) * n_dp < count
     inv_count = 1.0 / token_total.astype(f32)
+    ranks = lax.broadcasted_iota(jnp.int32, (1, 128), 1)
+    load = jnp.zeros((1, 128), jnp.int32)
+    for r in range(n_dp):
+        for m in range(micro):
+            off = n_dp - 1 - ranks if m % 2 else ranks
+            some = (fills_out[r, m : m + 1, :] - off + n_dp - 1) >> (n_dp.bit_length() - 1)
+            load = load + jnp.minimum(jnp.maximum(some, 0), share)
+    load = jnp.where(ranks < n_dp, load, 0)
+    steps = jnp.zeros((1, 128), jnp.int32)
+    for i in range(-(-rows // chunk)):
+        steps = steps + (load > i * chunk).astype(jnp.int32)
+    trips[0] = jnp.max(steps)
     live_f = live.astype(f32)
+    line = lax.broadcasted_iota(jnp.int32, (rows, rows), 0)
+    lane = lax.broadcasted_iota(jnp.int32, (rows, rows), 1)
     upto = (line < lane).astype(f32).astype(bf16)
     place = jnp.dot(
         jnp.broadcast_to(live_f, (16, rows)).astype(bf16), upto, preferred_element_type=f32
@@ -439,34 +497,42 @@
     top = n_dp
     partner = mine + 1 - 2 * core
     trees = {"h": (hbuf, ht_s, ht_r), "g": (gbuf, gt_s, gt_r)}
-    tree_copies = {}
+
+    def hop(k, t):
+        buf, s_sems, r_sems = trees[k]
+        if t >= nodes:
+            dp_o, mp_o = owner(t - nodes, mine, core)
+            device = {"mp": partner}
+        else:
+            dp_o, mp_o = owner(t & (t - 1), mine, core)
+            dp_t, mp_t = toward(t & -t)
+            device = {"dp": dp_t, "mp": mp_t}
+        block = buf.at[rank_rows(dp_o), strip(mp_o)]
+        return remote(block, block, s_sems.at[t], r_sems.at[t], device)
 
     def forward(k, t):
-        buf, s_sems, r_sems = trees[k]
-        dp_o, mp_o = owner(t, mine, core)
-        place_ = buf.at[rank_rows(dp_o), strip(mp_o)]
         bit = (t & -t) // 2 if t else top
         while bit >= 1:
-            dp_t, mp_t = toward(bit)
-            tree_copies[k, t ^ bit] = ship(
-                place_, place_, s_sems.at[t ^ bit], r_sems.at[t ^ bit], {"dp": dp_t, "mp": mp_t}
-            )
+            hop(k, t ^ bit).start()
             bit //= 2
-        tree_copies[k, nodes + t] = ship(
-            place_, place_, s_sems.at[nodes + t], r_sems.at[nodes + t], {"mp": partner}
-        )
+        hop(k, nodes + t).start()
 
     def arrive(k, *ts):
         for t in ts:
-            tree_copies[k, t].wait_recv()
+            hop(k, t).wait_recv()
             forward(k, t)
 
     def joined(k, z):
         for t in range(4 * z, 4 * z + 4):
-            tree_copies[k, nodes + t].wait_recv()
+            hop(k, nodes + t).wait_recv()
 
     def base_of(z):
-        return 2 * flipped_by(lax.div(me, 2), z)
+        at, out, bit = lax.div(me, 2), 0, 1
+        while bit < zs:
+            a, b = lax.rem(lax.div(at, bit), 2), lax.rem(lax.div(z, bit), 2)
+            out = out + bit * (a + b - 2 * a * b)
+            bit *= 2
+        return 2 * out
 
     half = lax.div(me, n_dp // n_mp)
     part_at = lax.rem(me, n_dp // n_mp)
@@ -480,59 +546,71 @@
     def rms(block):
         return lax.rsqrt(jnp.sum(block * block, axis=1, keepdims=True) / model + epsilon)
 
-    def do_pre(z):
-        joined("h", z)
+    tiles = [slice(n * tile, (n + 1) * tile) for n in range(ff // tile)]
+    mid = (len(tiles) + 1) // 2
+    pieces = [tiles[:mid], tiles[mid:]]
+
+    def keep(z, pairs, at):
+        held = pl.ds(pl.multiple_of(z * group, 64), group)
+        return [
+            pltpu.make_async_copy(ref.at[held, :], out.at[held, :], o_sem.at[at + n, z])
+            for n, (ref, out) in enumerate(pairs)
+        ]
+
+    def keep_pre(z):
+        return keep(z, ((act, act_o), (ns, ns_o)), 0)
+
+    def keep_grad(z):
+        return keep(z, ((gp, gp_o), (gs, gs_o)), 2)
+
+    def do_pre(z, between):
         base = base_of(z)
+        held = pl.ds(pl.multiple_of(z * group, 64), group)
 
         def norm_rows(i, carry):
-            src = pl.ds(pl.multiple_of(base * chunk + i * 16, 16), 16)
-            dst = pl.ds(pl.multiple_of(i * 16, 16), 16)
-            value = hbuf[src, :].astype(f32)
-            normed[dst, :] = (value * rms(value) * gain_full[0:1, :]).astype(bf16)
+            for k in range(4):
+                src = pl.ds(pl.multiple_of(base * chunk + i * 64 + k * 16, 16), 16)
+                dst = pl.ds(pl.multiple_of(i * 64 + k * 16, 16), 16)
+                value = hbuf[src, :].astype(f32)
+                normed[dst, :] = (value * rms(value) * gain_full[0:1, :]).astype(bf16)
             return carry
 
-        lax.fori_loop(0, group // 16, norm_rows, 0)
-        nsl[z] = slice_cols(normed[:, strip(half)].astype(f32)).astype(bf16)
-
-        def pre_tile(n, carry):
-            at = pl.ds(pl.multiple_of(n * tile, tile), tile)
-            value = jnp.dot(normed[...], upw[:, at], preferred_element_type=f32)
-            pre[z, :, at] = value
-            bent = jnp.tanh(gelu_slope * (value + gelu_cube * (value * value * value)))
-            act[z, :, at] = (value * (0.5 * (1.0 + bent))).astype(bf16)
-            return carry
-
-        lax.fori_loop(0, ff // tile, pre_tile, 0)
-
-    def do_grad(z):
-        joined("g", z)
+        with phase("norm"):
+            lax.fori_loop(0, group // 64, norm_rows, 0)
+            ns[held, :] = slice_cols(normed[:, strip(half)].astype(f32)).astype(bf16)
+        for n, some in enumerate(pieces):
+            between(n)
+            with phase("pre_tiles"):
+                for at in some:
+                    value = jnp.dot(normed[...], upw[:, at], preferred_element_type=f32)
+                    pre[z, :, at] = value
+                    bent = jnp.tanh(
+                        gelu_slope * (value + gelu_cube * (value * value * value))
+                    )
+                    act[held, at] = (value * (0.5 * (1.0 + bent))).astype(bf16)
+        for copy in keep_pre(z):
+            copy.start()
+
+    def do_grad(z, between):
         base = base_of(z)
         block = pl.ds(pl.multiple_of(base * chunk, 16), group)
-        gsl[...] = slice_cols(gbuf[block, strip(half)].astype(f32)).astype(bf16)
-
-        def grad_tile(n, carry):
-            at = pl.ds(pl.multiple_of(n * tile, tile), tile)
-            grad = contract_cols(gbuf[block, :], dnw[at, :])
-            value = pre[z, :, at]
-            square = value * value
-            bent = jnp.tanh(gelu_slope * (value + gelu_cube * (square * value)))
-            slope = 0.5 * (1.0 + bent) + (0.5 * value) * (1.0 - bent * bent) * (
-                gelu_slope * (1.0 + 3.0 * gelu_cube * square)
-            )
-            back = (grad * slope).astype(bf16)
-            if z == 0:
-                gp_own[:, at] = back
-            up_term = contract_rows(nsl[z], back)
-            down_term = contract_rows(act[z, :, at], gsl[...])
-            if z == 0:
-                up_out[:, at] = up_term
-                down_out[at, :] = down_term
-            else:
-                up_out[:, at] += up_term
-                down_out[at, :] += down_term
-            return carry
-
-        lax.fori_loop(0, ff // tile, grad_tile, 0)
+        held = pl.ds(pl.multiple_of(z * group, 64), group)
+        with phase("gslice"):
+            gs[held, :] = slice_cols(gbuf[block, strip(half)].astype(f32)).astype(bf16)
+        for n, some in enumerate(pieces):
+            between(n)
+            with phase("grad_tiles"):
+                for at in some:
+                    grad = jnp.dot(gbuf[block, :], dnt[:, at], preferred_element_type=f32)
+                    value = pre[z, :, at]
+                    square = value * value
+                    bent = jnp.tanh(gelu_slope * (value + gelu_cube * (square * value)))
+                    slope = 0.5 * (1.0 + bent) + (0.5 * value) * (1.0 - bent * bent) * (
+                        gelu_slope * (1.0 + 3.0 * gelu_cube * square)
+                    )
+                    gp[held, at] = (grad * slope).astype(bf16)
+        for copy in keep_grad(z):
+            copy.start()
 
     def compact(got, buf, scale):
         packed = jnp.dot(pick[...], got[...], preferred_element_type=f32)
@@ -540,87 +618,136 @@
             packed = packed * scale
         buf[rank_rows(me), strip(mine)] = packed.astype(bf16)
 
-    for copy in h_copies:
-        copy.wait_recv()
-    compact(got_h, hbuf, None)
-    forward("h", 0)
-    for copy in gain_copies:
-        copy.wait_recv()
-    arrive("h", 8, 4, 2, 1)
-    for copy in g_copies:
-        copy.wait_recv()
-    compact(got_g, gbuf, inv_count)
-    forward("g", 0)
-    arrive("h", 12, 3, 6, 10)
-    loads[0].wait()
-    do_pre(0)
-    arrive("h", 14, 5, 7)
-    arrive("g", 8, 4)
-    do_pre(1)
-    arrive("h", 9, 11)
-    arrive("g", 2, 1)
-    do_pre(2)
-    arrive("h", 13, 15)
-    arrive("g", 12)
-    do_pre(3)
-    arrive("g", 3, 6, 10)
-    loads[1].wait()
-    do_grad(0)
-
     own = pl.ds(pl.multiple_of(low * chunk, 16), chunk)
-    own_gp = gp_own[own, :]
-    own_pre = pre[0, own, :]
-    inv_rms = rms(hbuf[rank_rows(me), :].astype(f32))
-    row_part = jnp.sum(own_gp.astype(f32) * own_pre, axis=1, keepdims=True)
-    row_send[...] = jnp.broadcast_to(row_part / inv_rms, row_send.shape)
-
-    def part_tile(n, carry):
-        at = pl.ds(pl.multiple_of(n * tile, tile), tile)
-        part[:, at] = contract_cols(gp_own[own, :], upw[at, :]).astype(bf16)
+
+    def own_parts():
+        own_gp = gp[own, :]
+        row_part = jnp.sum(own_gp.astype(f32) * pre[0, own, :], axis=1, keepdims=True)
+        inv_rms = rms(hbuf[rank_rows(me), :].astype(f32))
+        row_send[...] = jnp.broadcast_to(row_part / inv_rms, row_send.shape)
+        for n in range(model // tile):
+            at = slice(n * tile, (n + 1) * tile)
+            if n % 7 == 0:
+                run(own_events[n // 7])
+            with phase("part_tiles"):
+                part[:, at] = contract_cols(gp[own, :], upw[at, :]).astype(bf16)
+        start(part_copies)
+
+    def own_rows():
+        with phase("part_wait"):
+            received(part_copies)
+        inv_rms = rms(hbuf[rank_rows(me), :].astype(f32))
+        grad_normed = part[:, strip(mine)].astype(f32)
+        row_dot = row_send[:, 0:1]
+        for d in range(1, n_mp):
+            peer = lax.rem(mine + d, n_mp)
+            grad_normed = grad_normed + shares[peer].astype(f32)
+            row_dot = row_dot + rows_in[peer][:, 0:1]
+        values = hbuf[rank_rows(me), strip(mine)].astype(f32)
+        scaled = gbuf[rank_rows(me), strip(mine)].astype(f32)
+        cubed = inv_rms * inv_rms * inv_rms
+        in_rows = (
+            scaled + gain_row * grad_normed * inv_rms - values * (cubed * row_dot / model)
+        ).astype(bf16)
+        gain_term = jnp.sum(grad_normed * values * inv_rms, axis=0, keepdims=True)
+        term_send[...] = jnp.broadcast_to(gain_term, term_send.shape)
+        terms_in[me] = term_send[...]
+        sent_back[...] = contract_rows(pick[...], in_rows).astype(bf16)
+        got_back[here, :] = sent_back[here, :]
+        start(back_copies)
+
+    with phase("h_wait"):
+        received(h_copies)
+    with phase("start_h"):
+        compact(got_h, hbuf, None)
+        forward("h", 0)
+    with phase("gain_wait"):
+        received(gain_copies)
+
+    def begin_g():
+        start(g_copies)
+        got_g[here, :] = sent_g[here, :]
+
+    def pack_g():
+        with phase("g_wait"):
+            received(g_copies)
+        with phase("start_g"):
+            compact(got_g, gbuf, inv_count)
+            forward("g", 0)
+
+    def run(events):
+        for event in events:
+            if callable(event):
+                event()
+            elif event[0] == "j":
+                with phase("join_" + event):
+                    joined(event[1], int(event[2:]))
+            else:
+                with phase(event):
+                    arrive(event[0], int(event[1:]))
+
+    own_events = (["g10", "g6"], ["g5", "g9"])
+    pre_events = {
+        0: (["h2", "h1", "h4", "h8", begin_g, "h3", up_load.wait, "jh0"], ["h12"], []),
+        1: (["h10", "h6", "h5", "h9", pack_g, "h7", "jh1"], ["h14"], ["g2", "g1"]),
+        2: (["jh2"], ["g14"], ["g7"]),
+        3: (["g11", "jh3"], ["g13"], ["g15"]),
+    }
+    grad_events = {
+        0: (["g8", "g4", "h11", "h13", "g3", "jg0"], ["h15"], ["g12"]),
+        1: (["jg1"], [], []),
+        2: ([own_rows, "jg2"], [], []),
+        3: (["jg3"], [], []),
+    }
+
+    def at_step(table, i, n):
+        for z in range(zs):
+            if table[z][n]:
+                pl.when(i == z)(lambda z=z: run(table[z][n]))
+
+    turn = zs // 2
+
+    def step(i, carry):
+        @pl.when(jnp.logical_or(i < turn, jnp.logical_and(i > turn, i <= zs)))
+        def _():
+            z = i - i // (turn + 1)
+            at_step(pre_events, z, 0)
+            do_pre(z, lambda n: at_step(pre_events, z, n + 1))
+
+        @pl.when(jnp.logical_or(i == turn, i > zs))
+        def _():
+            z = (i - turn) * (i // (zs + 1)) - turn * (i // (zs + 1))
+            at_step(grad_events, z, 0)
+            do_grad(z, lambda n: at_step(grad_events, z, n + 1))
+
+            @pl.when(i == turn)
+            def _():
+                own_parts()
+
         return carry
 
-    lax.fori_loop(0, model // tile, part_tile, 0)
-    part_copies = to_mp(lambda peer: part.at[:, strip(peer)], shares.at[mine], p_s, p_r)
-    part_copies += to_mp(lambda peer: row_send, rows_in.at[mine], q_s, q_r)
-
-    arrive("g", 14, 5, 7)
-    do_grad(1)
-
-    for copy in part_copies:
-        copy.wait_recv()
-    grad_normed = part[:, strip(mine)].astype(f32)
-    row_dot = row_send[:, 0:1]
-    for d in range(1, n_mp):
-        peer = lax.rem(mine + d, n_mp)
-        grad_normed = grad_normed + shares[peer].astype(f32)
-        row_dot = row_dot + rows_in[peer][:, 0:1]
-    values = hbuf[rank_rows(me), strip(mine)].astype(f32)
-    scaled = gbuf[rank_rows(me), strip(mine)].astype(f32)
-    cubed = inv_rms * inv_rms * inv_rms
-    in_rows = (
-        scaled + gain[...] * grad_normed * inv_rms - values * (cubed * row_dot / model)
-    ).astype(bf16)
-    gain_term = jnp.sum(grad_normed * values * inv_rms, axis=0, keepdims=True)
-    term_send[...] = jnp.broadcast_to(gain_term, term_send.shape)
-    terms_in[me] = term_send[...]
-    back = contract_rows(pick[...], in_rows).astype(bf16)
-    sent_back[...] = back
-    got_back[here, :] = sent_back[here, :]
-    back_copies = to_dp(lambda peer: slot(sent_back, peer), slot(got_back, me), b_s, b_r)
-    back_copies += to_dp(lambda peer: term_send, terms_in.at[me], t_s, t_r)
-
-    arrive("g", 9, 11)
-    do_grad(2)
-    arrive("g", 13, 15)
-    do_grad(3)
-
-    for copy in back_copies:
-        copy.wait_recv()
-    gain_out[...] = jnp.sum(terms_in[...], axis=0)
-    for m in range(micro):
-        in_part[m] = contract_rows(perm[:, m * tok : (m + 1) * tok], got_back[...]).astype(bf16)
-    for copy in sent:
-        copy.wait_send()
+    lax.fori_loop(0, 2 * zs, step, 0)
+
+    with phase("back_wait"):
+        received(back_copies)
+    lasts = [
+        pltpu.make_async_copy(got_back, back_o, o_sem.at[4, 0]),
+        pltpu.make_async_copy(terms_in, terms_o, o_sem.at[4, 1]),
+    ]
+    start(lasts)
+    with phase("keeps_wait"):
+        for z in range(zs):
+            for copy in keep_pre(z) + keep_grad(z):
+                copy.wait()
+        for copy in lasts:
+            copy.wait()
+    with phase("sends_wait"):
+        for copies in (fill_copies, h_copies, gain_copies, g_copies, part_copies, back_copies):
+            for copy in copies:
+                copy.wait_send()
+        for k in ("h", "g"):
+            for t in range(1, 2 * nodes):
+                hop(k, t).wait_send()
 
 
 def fused_call(hidden_in, out_grad, pack_fill, norm_gain, index, up_weight, down_weight):
@@ -641,29 +768,32 @@
     return pl.pallas_call(
         fused_kernel,
         out_shape=[
-            jax.ShapeDtypeStruct((micro, tok, width), bf16),
-            jax.ShapeDtypeStruct((cols, ff), f32),
-            jax.ShapeDtypeStruct((ff, cols), f32),
-            jax.ShapeDtypeStruct((8, width), f32),
-            jax.ShapeDtypeStruct((n_dp, 8, 128), jnp.int32),
+            jax.ShapeDtypeStruct((zs * group, ff), bf16),
+            jax.ShapeDtypeStruct((zs * group, ff), bf16),
+            jax.ShapeDtypeStruct((zs * group, cols), bf16),
+            jax.ShapeDtypeStruct((zs * group, cols), bf16),
+            jax.ShapeDtypeStruct((rows, width), bf16),
+            jax.ShapeDtypeStruct((n_dp, 8, width), f32),
+            jax.ShapeDtypeStruct((1,), jnp.int32),
         ],
         in_specs=[vmem, vmem, smem, vmem, smem, hbm, hbm],
-        out_specs=[vmem] * 5,
+        out_specs=[hbm] * 6 + [smem],
         scratch_shapes=[
             pltpu.VMEM((model, ff), bf16),
-            pltpu.VMEM((ff, model), bf16),
+            pltpu.VMEM((model, ff), bf16),
             pltpu.VMEM((n_dp * chunk, model), bf16),
             pltpu.VMEM((n_dp * chunk, model), bf16),
-            pltpu.VMEM((zs, group, ff), bf16),
+            pltpu.VMEM((zs * group, ff), bf16),
             pltpu.VMEM((zs, group, ff), f32),
             pltpu.VMEM((group, model), bf16),
-            pltpu.VMEM((zs, group, cols), bf16),
-            pltpu.VMEM((group, cols), bf16),
-            pltpu.VMEM((group, ff), bf16),
+            pltpu.VMEM((zs * group, cols), bf16),
+            pltpu.VMEM((zs * group, cols), bf16),
+            pltpu.VMEM((zs * group, ff), bf16),
             pltpu.VMEM((rows, width), bf16),
             pltpu.VMEM((rows, width), bf16),
             pltpu.VMEM((rows, width), bf16),
             pltpu.VMEM((rows, width), bf16),
+            pltpu.VMEM((n_dp, 8, 128), jnp.int32),
             pltpu.VMEM((8, 128), jnp.int32),
             pltpu.VMEM((8, width), f32),
             pltpu.VMEM((8, model), f32),
@@ -677,7 +807,8 @@
             pltpu.VMEM((rows, width), bf16),
             pltpu.VMEM((rows, rows), bf16),
             pltpu.VMEM((chunk, rows), bf16),
-            dma((2,)),
+            dma((8,)),
+            dma((5, zs)),
         ]
         + [dma((n_dp,))] * 6
         + [dma((n_mp,))] * 2
@@ -690,36 +821,78 @@
         cost_estimate=pl.CostEstimate(
             flops=8 * rows * model * ff, bytes_accessed=6 * model * ff, transcendentals=0
         ),
-    )(hidden_in, out_grad, pack_fill, norm_gain[None, :], index, up_weight, down_weight)
+    )(hidden_in, out_grad, pack_fill.T, norm_gain, index, up_weight, down_weight)
+
+
+def finish_kernel(
+    act, gp, ns, gs, back, terms, in_part, up_out, down_out, gain_out, nst, gst
+):
+    @pl.when(pl.program_id(0) == 0)
+    def _():
+        nst[...] = ns[...].T
+        gst[...] = gs[...].T
+        micro, tok, width = in_part.shape
+        n_dp = terms.shape[0]
+        perm = dealing(micro, tok, n_dp)
+        for m in range(micro):
+            in_part[m] = contract_rows(perm[:, m * tok : (m + 1) * tok], back[...]).astype(
+                jnp.bfloat16
+            )
+        gain_out[...] = jnp.sum(terms[...], axis=0)[0:1].reshape(width)
+
+    up_out[...] = jnp.dot(nst[...], gp[...], preferred_element_type=jnp.float32)
+    down_out[...] = jnp.dot(gst[...], act[...], preferred_element_type=jnp.float32)
+
+
+def finish_call(act, gp, ns, gs, back, terms, micro):
+    total, ff = act.shape
+    cols = ns.shape[1]
+    rows, width = back.shape
+    tok = rows // micro
+    tile = 256
+    f32, bf16 = jnp.float32, jnp.bfloat16
+
+    def whole(shape):
+        return pl.BlockSpec(shape, lambda n: (0,) * len(shape))
+
+    def strips(height):
+        return pl.BlockSpec((height, tile), lambda n: (0, n))
+
+    return pl.pallas_call(
+        finish_kernel,
+        grid=(ff // tile,),
+        out_shape=[
+            jax.ShapeDtypeStruct((micro, tok, width), bf16),
+            jax.ShapeDtypeStruct((cols, ff), f32),
+            jax.ShapeDtypeStruct((cols, ff), f32),
+            jax.ShapeDtypeStruct((width,), f32),
+        ],
+        in_specs=[
+            strips(total), strips(total), whole(ns.shape), whole(gs.shape),
+            whole(back.shape), whole(terms.shape),
+        ],
+        out_specs=[whole((micro, tok, width)), strips(cols), strips(cols), whole((width,))],
+        scratch_shapes=[pltpu.VMEM((cols, total), bf16), pltpu.VMEM((cols, total), bf16)],
+        compiler_params=pltpu.CompilerParams(vmem_limit_bytes=67043328),
+    )(act, gp, ns, gs, back, terms)
 
 
 def on_device_fused(hidden_in, out_grad, pack_fill, norm_gain, up_weight, down_weight):
-    micro, tok, _ = hidden_in.shape
-    n_dp = lax.axis_size("dp")
-    share = tok // n_dp
-    chunk = packed_chunk(micro * tok)
-
     def run_chunk(index):
-        return fused_call(
+        *parts, trips = fused_call(
             hidden_in, out_grad, pack_fill, norm_gain,
             jnp.reshape(index, (1,)).astype(jnp.int32), up_weight, down_weight,
         )
-
-    *total, fills = run_chunk(jnp.int32(0))
-    fills = fills[:, :micro, 0].T
-    odd = (jnp.arange(micro, dtype=jnp.int32) % 2).reshape(1, micro, 1)
-    ranks = jnp.arange(n_dp, dtype=jnp.int32)[:, None, None]
-    starts = jnp.where(odd == 1, n_dp - 1 - ranks, ranks)
-    counts = jnp.clip((fills[None] - starts + n_dp - 1) // n_dp, 0, share)
-    most = jnp.max(jnp.sum(counts, axis=(1, 2)))
-    chunk_total = (most + chunk - 1) // chunk
+        return finish_call(*parts, hidden_in.shape[0]), trips
+
+    total, trips = run_chunk(jnp.int32(0))
 
     def add_chunk(index, so_far):
-        *more, _ = run_chunk(index)
+        more, _ = run_chunk(index)
         return jax.tree.map(jnp.add, so_far, more)
 
-    in_grad, up_grad, down_grad, gain = lax.fori_loop(1, chunk_total, add_chunk, total)
-    return (in_grad, up_grad, down_grad, gain[0])
+    in_grad, up_grad, down_grad, gain = lax.fori_loop(1, trips[0], add_chunk, total)
+    return (in_grad, up_grad, down_grad.T, gain)
 
 
 def solution(mesh):

time: 152 us -> 116 us (0.76)
  Pallas kernels: 133 us -> 114 us
  local copies, waits for them, and re-layouts: 14.7 us -> 0 us
  other arithmetic: 2.15 us -> 0 us
    pallas_call x1 -> x2, Pallas kernels: 133 us -> 114 us  [the longest x1 104 us: fused_call(): pl.pallas_call(fused_kernel, out_shape=[jax.ShapeDtypeStruct((zs * group,...]
    unnamed x6 -> x0, local copies, waits for them, and re-layouts: 9.99 us -> none
    broadcast_in_dim x2 -> x0, local copies, waits for them, and re-layouts: 2.53 us -> none  [fused_call(): norm_gain[None, :]]
    slice x3 -> x0, local copies, waits for them, and re-layouts: 2.21 us -> none  [the longest x1 1.35 us: on_device_fused(): return (in_grad, up_grad, down_grad, gain[0])]
where the time goes in v2:
time: 116 us; the launch traced here: 115 us
  Pallas kernels  114 us (98%)
    pallas_call x1, Pallas kernels, fused_call(): pl.pallas_call(fused_kernel, out_shape=[jax.ShapeDtypeStruct((zs * group,...  104 us
    pallas_call x1, Pallas kernels, finish_call(): pl.pallas_call(finish_kernel, grid=(ff // tile,), out_shape=[jax.ShapeDty...  9.88 us

profile of v2, /device:TPU:0, one launch (start us, length us, event | category | flops | bytes accessed | tf_op | source)
XLA Modules:
  0.0 115.1 jit_solution(7865706014051837373)
XLA Ops:
  0.6 103.8 %shard_map.93 = (bf16[768,1792]{1,0:T(8,128)(2,1)}, bf16[768,1792]{1,0:T(8,128)(2,1)}, bf16[768,448]{1,0:T(8,128)(2,1)}, bf16[768,448]{1,0:T(8,128)(2,1)}, bf16[...) custom-call(bf16[2,128,896]{2,1,0:T(8,128)(2,1)} %hid.1, bf16[2,128,896]{2,1,0:T(8,128)(2,1)} %og.1, ...), custom_call_target="tpu_custom_call" | custom-call | flops 13153337344 | bytes 38535168 | tf_op jit(solution)/shard_map/pallas_call | solution.py:768
  104.5 9.9 %shard_map.94 = (bf16[2,128,896]{2,1,0:T(8,128)(2,1)}, f32[448,1792]{1,0:T(8,128)}, f32[448,1792]{1,0:T(8,128)}, f32[896]{0:T(1024)}) custom-call(bf16[768,1792]{1,0:T(8,128)(2,1)} %get-tuple-element.91.act, bf16[768,1792]{1,0:T(8,128)(2,1)} %get-tuple-element.92.gp, bf16[768,448]{1,0:T(8,128)(2,1)} %get-tuple-element.93.ns, ...), custom_call_target="tpu_custom_call" | custom-call | tf_op jit(solution)/shard_map/pallas_call | solution.py:861
  114.3 0.6 while.16
